TPU v7x, 8 devices: a whole 2x2x1 slice. The times are simulated.
8 devices in a mesh: dp: 2 (over z, y), sp: 4 (over x, core).
Axes of the slice: x: 2, y: 2, z: 1, core: 2. Of those that a mesh axis runs over, the one named last changes fastest.
Arguments:
- pair_rep: float32 [256, 128, 128], P(('dp', 'sp')), parts along dimension 0
- w_qkvg_s: bfloat16 [128, 512], replicated
- w_bias_s: bfloat16 [4, 128], replicated
- w_out_s: bfloat16 [128, 128], replicated
- w_qkvg_e: bfloat16 [128, 512], replicated
- w_bias_e: bfloat16 [4, 128], replicated
- w_out_e: bfloat16 [128, 128], replicated
- w_one: bfloat16 [128, 512], replicated
- w_two: bfloat16 [512, 128], replicated
Outputs:
- output: float32 [256, 128, 128], P(('dp', 'sp')), parts along dimension 0
There are 2 independent parts. A program takes and returns all parts, laid end to end along the dimension named above; an argument that names none is the same for every part.
All inputs are finite; a program needn't handle non-finite values.
Results may differ from a plain program's by a relative error of at most 0.00995982.
Values are sent between devices in bfloat16 or wider.
A program may use at most 1 GiB of HBM per device.

v0:
```python
import jax
import jax.numpy as jnp
from jax import lax
from jax.sharding import PartitionSpec as P

LN_EPS = 1e-5
SCORE_CAP = 2 ** 23


def layer_norm(values):
    vals_f = values.astype(jnp.float32)
    mean_c = jnp.mean(vals_f, axis=-1, keepdims=True)
    centered = vals_f - mean_c
    variance = jnp.mean(centered * centered, axis=-1, keepdims=True)
    return (centered * lax.rsqrt(variance + LN_EPS)).astype(jnp.bfloat16)


def project(normed, w_qkvg, num_heads):
    channels = w_qkvg.shape[0]
    projected = jnp.dot(normed, w_qkvg, preferred_element_type=jnp.float32)
    split_shape = normed.shape[:-1] + (num_heads, channels // num_heads)
    queries = projected[..., :channels].astype(jnp.bfloat16).reshape(split_shape)
    key_vecs = projected[..., channels:2 * channels].astype(jnp.bfloat16).reshape(split_shape)
    val_vecs = projected[..., 2 * channels:3 * channels].astype(jnp.bfloat16).reshape(split_shape)
    gate_vals = jax.nn.sigmoid(projected[..., 3 * channels:]).reshape(split_shape)
    return queries, key_vecs, val_vecs, gate_vals


def attend(queries, key_vecs, val_vecs, gate_vals, bias_full, w_out, score_form, mix_form):
    head_dim = queries.shape[-1]
    scores = jnp.einsum(score_form, queries, key_vecs, preferred_element_type=jnp.float32)
    scores = scores * head_dim ** -0.5 + bias_full.astype(jnp.float32)
    attn_prob = jax.nn.softmax(scores, axis=-1).astype(jnp.bfloat16)
    attn_out = jnp.einsum(mix_form, attn_prob, val_vecs, preferred_element_type=jnp.float32)
    gated_out = (attn_out * gate_vals).astype(jnp.bfloat16)
    merged = gated_out.reshape(gated_out.shape[:-2] + (w_out.shape[0],))
    return jnp.dot(merged, w_out, preferred_element_type=jnp.float32)


def transition(resid_in, w_one, w_two):
    hidden = jax.nn.relu(jnp.dot(layer_norm(resid_in), w_one, preferred_element_type=jnp.float32))
    return jnp.dot(hidden.astype(jnp.bfloat16), w_two, preferred_element_type=jnp.float32)


def block_size(total_len, per_item):
    return max(candidate for candidate in range(1, total_len + 1) if total_len % candidate == 0 and (candidate == 1 or candidate * per_item <= SCORE_CAP))


def solution(mesh):
    row_spec = P(('dp', 'sp'), None, None)

    def local_fn(pair_loc, w_qkvg_s, w_bias_s, w_out_s, w_qkvg_e, w_bias_e, w_out_e, w_one, w_two):
        num_rows, seq_len, channels = pair_loc.shape
        num_heads = w_bias_s.shape[0]
        blk_rows = block_size(num_rows, num_heads * seq_len * seq_len)
        normed = layer_norm(pair_loc)
        bias_loc = jnp.einsum('hc,jkc->hjk', w_bias_s, normed, preferred_element_type=jnp.float32).astype(jnp.bfloat16)
        bias_s = lax.all_gather(bias_loc, 'sp', axis=1, tiled=True)

        def start_block(block_idx):
            normed_blk = lax.dynamic_slice_in_dim(normed, block_idx * blk_rows, blk_rows, axis=0)
            queries, key_vecs, val_vecs, gate_vals = project(normed_blk, w_qkvg_s, num_heads)
            return attend(queries, key_vecs, val_vecs, gate_vals, bias_s, w_out_s, 'rjhd,rkhd->rhjk', 'rhjk,rkhd->rjhd')

        start_upd = lax.map(start_block, jnp.arange(num_rows // blk_rows))
        pair_one = pair_loc + start_upd.reshape(num_rows, seq_len, channels)
        col_major = lax.all_to_all(pair_one.astype(jnp.bfloat16), 'sp', 1, 0, tiled=True)
        normed_c = layer_norm(col_major)
        bias_loc_e = jnp.einsum('hc,kic->hik', w_bias_e, normed_c, preferred_element_type=jnp.float32).astype(jnp.bfloat16)
        bias_e = lax.all_gather(bias_loc_e, 'sp', axis=1, tiled=True)

        def end_block(block_idx):
            normed_blk = lax.dynamic_slice_in_dim(normed_c, block_idx * blk_rows, blk_rows, axis=1)
            pair_blk = lax.dynamic_slice_in_dim(col_major, block_idx * blk_rows, blk_rows, axis=1)
            queries, key_vecs, val_vecs, gate_vals = project(normed_blk, w_qkvg_e, num_heads)
            end_upd = attend(queries, key_vecs, val_vecs, gate_vals, bias_e, w_out_e, 'ijhd,kjhd->jhik', 'jhik,kjhd->ijhd')
            pair_two = pair_blk.astype(jnp.float32) + end_upd
            return (end_upd + transition(pair_two, w_one, w_two)).astype(jnp.bfloat16)

        delta_blocks = lax.map(end_block, jnp.arange(num_rows // blk_rows))
        delta_cols = jnp.moveaxis(delta_blocks, 0, 1).reshape(seq_len, num_rows, channels)
        delta_rows = lax.all_to_all(delta_cols, 'sp', 0, 1, tiled=True)
        return pair_one + delta_rows.astype(jnp.float32)

    return jax.shard_map(local_fn, mesh=mesh, in_specs=(row_spec, P(), P(), P(), P(), P(), P(), P(), P()), out_specs=row_spec, check_vma=False)
```

profile of v0, /device:TPU:0, one launch (start us, length us, event | category | flops | bytes accessed | tf_op | source)
XLA Modules:
  0.0 137.2 jit_solution(5341797975510322616)
XLA Ops:
  0.0 2.4 %reduce_sum.76 = f32[32,128]{1,0:T(8,128)S(1)} reduce(f32[32,128,128]{2,1,0:T(8,128)} %param.9, f32[]{:T(128)} %constant.38.clone.1), dimensions={2}, to_apply=%region_0.0 | reduce | flops 520192 | bytes 2113540 | tf_op jit(solution)/shard_map/reduce_sum | solution.py:12
  3.7 3.4 %fusion.54 = (bf16[32,128,512]{2,1,0:T(8,128)(2,1)}, f32[32,128,512]{2,1,0:T(8,128)S(1)}) fusion(bf16[128,512]{1,0:T(8,128)(2,1)S(1)} %copy-done, f32[32,128,128]{2,1,0:T(8,128)S(1)} %copy-done.2, f32[32,128]{1,0:T(8,128)S(1)} %add_rsqrt_fusion.1, f32[32,128]{1,0:T(8,128)S(1)} %broadcast_multiply_fusion.1), kind=kOutput, calls=%fused_computation.80 | convolution fusion | flops 540540928 | bytes 14843904 | tf_op jit(solution)/shard_map/while/body/eval_jaxpr/dot_general | solution.py:20
  7.1 1.9 %fusion.19 = f32[32,128,128]{2,1,0:T(8,128)} fusion(f32[32,128,512]{2,1,0:T(8,128)S(1)} %get-tuple-element.50), kind=kLoop, calls=%fused_computation.27 | loop fusion | flops 1572864 | bytes 4194304 | tf_op jit(solution)/shard_map/while/body/eval_jaxpr/div | solution.py:25
  9.0 3.0 %copy.165 = f32[32,128,128]{1,2,0:T(8,128)} copy(f32[32,128,128]{2,1,0:T(8,128)} %fusion.19) | data formatting | bytes 4194304 | tf_op jit(solution)/shard_map/while/body/eval_jaxpr/div | solution.py:25
  11.9 3.6 %fusion.53 = (bf16[32,128,128]{2,1,0:T(8,128)(2,1)S(1)}, bf16[32,128,128]{2,1,0:T(8,128)(2,1)}, bf16[32,128,128]{2,1,0:T(8,128)(2,1)}) fusion(bf16[32,128,512]{2,1,0:T(8,128)(2,1)} %get-tuple-element.49), kind=kLoop, calls=%fused_computation.79 | loop fusion | bytes 6291456 | tf_op jit(solution)/shard_map/while/body/eval_jaxpr/slice | solution.py:23
  15.5 2.3 %copy.159 = bf16[32,128,128]{1,2,0:T(8,128)(2,1)} copy(bf16[32,128,128]{2,1,0:T(8,128)(2,1)} %get-tuple-element.46) | data formatting | bytes 2097152 | tf_op jit(solution)/shard_map/while/body/eval_jaxpr/slice | solution.py:24
  17.8 1.4 %fusion.23 = bf16[4,32,128]{2,0,1:T(4,128)(2,1)S(1)} fusion(f32[32,128,128]{2,1,0:T(8,128)S(1)} %copy-done.2, f32[32,128]{1,0:T(8,128)S(1)} %add_rsqrt_fusion.1, f32[32,128]{1,0:T(8,128)S(1)} %broadcast_multiply_fusion.1, bf16[4,128]{1,0:T(4,128)(2,1)S(1)} %copy-done.14), kind=kOutput, calls=%fused_computation.46 | convolution fusion | flops 5783552 | bytes 2163712 | tf_op jit(solution)/shard_map/hc,jkc->hjk/dot_general | solution.py:57
  19.2 10.3 %all_gather.6 = bf16[4,128,128]{2,0,1:T(4,128)(2,1)S(1)} all-gather(bf16[4,32,128]{2,0,1:T(4,128)(2,1)S(1)} %fusion.23), channel_id=1, replica_groups=mesh['dp'=2,'sp'=4] {'sp'}, dimensions={1}, use_global_device_ids=true | all-gather | bytes 163840 | tf_op jit(solution)/shard_map/all_gather | solution.py:58
  30.4 2.3 %copy.160 = bf16[32,128,128]{1,2,0:T(8,128)(2,1)} copy(bf16[32,128,128]{2,1,0:T(8,128)(2,1)} %get-tuple-element.45) | data formatting | bytes 2097152 | tf_op jit(solution)/shard_map/while/body/eval_jaxpr/slice | solution.py:22
  32.7 1.3 copy.161
  34.0 8.0 %fusion.55 = (f32[32,4,128]{2,1,0:T(4,128)S(1)}, f32[32,4,128,128]{2,3,1,0:T(8,128)}) fusion(f32[4,128,128]{1,2,0:T(8,128)S(1)} %copy-done.8, bf16[32,128,4,32]{1,3,2,0:T(8,128)(2,1)} %bitcast.96, bf16[32,128,4,32]{1,3,2,0:T(8,128)(2,1)} %bitcast.98), kind=kOutput, calls=%fused_computation.81 | convolution fusion | flops 142606464 | bytes 10813440 | tf_op jit(solution)/shard_map/while/body/eval_jaxpr/sub | solution.py:33
  42.0 5.2 %fusion.21 = bf16[32,128,4,32]{1,3,2,0:T(8,128)(2,1)S(1)} fusion(f32[32,128,4,32]{1,3,2,0:T(8,128)} %bitcast.92, bf16[32,128,4,32]{1,3,2,0:T(8,128)(2,1)S(1)} %bitcast.95, f32[32,4,128,128]{2,3,1,0:T(8,128)} %get-tuple-element.62, f32[32,4,128]{2,1,0:T(4,128)S(1)} %get-tuple-element.60), kind=kOutput, calls=%fused_computation.34 | convolution fusion | flops 139460608 | bytes 12648448 | tf_op jit(solution)/shard_map/while/body/eval_jaxpr/rhjk,rkhd->rjhd/dot_general | solution.py:34
  47.2 1.8 %fusion.56 = (bf16[32,128,128]{2,1,0:T(8,128)(2,1)S(1)}, f32[32,128,128]{2,1,0:T(8,128)}) fusion(f32[32,128,128]{2,1,0:T(8,128)S(1)} %copy-done.2, bf16[32,128,128]{1,2,0:T(8,128)(2,1)S(1)} %bitcast.100, bf16[128,128]{1,0:T(8,128)(2,1)S(1)} %copy-done.12), kind=kOutput, calls=%fused_computation.82 | convolution fusion | flops 135266304 | bytes 6324224 | tf_op jit(solution)/shard_map/while/body/eval_jaxpr/dot_general | solution.py:37
  49.7 16.9 %all_to_all.8 = bf16[32,128,128]{2,0,1:T(8,128)(2,1)S(1)} all-to-all(bf16[32,128,128]{2,0,1:T(8,128)(2,1)S(1)} %copy.167), channel_id=1, replica_groups=mesh['dp'=2,'sp'=4] {'sp'}, dimensions={1} | all-to-all | bytes 2097152 | tf_op jit(solution)/shard_map/all_to_all | solution.py:67
  67.2 1.9 %copy.188 = f32[128,32,128]{0,2,1:T(8,128)} copy(f32[128,32,128]{2,1,0:T(8,128)S(1)} %bitcast.87) | data formatting | bytes 4194304 | tf_op jit(solution)/shard_map/convert_element_type | solution.py:11
  69.9 1.3 multiply_reduce_fusion.1
  71.3 1.5 %multiply_convert_fusion.1 = bf16[128,32,128]{2,1,0:T(8,128)(2,1)S(1)} fusion(f32[128,32]{1,0:T(8,128)S(1)} %bitcast.102, f32[128,32]{1,0:T(8,128)S(1)} %bitcast.101, f32[4,32,32,128]{3,2,1,0:T(8,128)S(1)} %copy.169), kind=kLoop, calls=%fused_computation.38 | loop fusion | flops 1572864 | bytes 3178496 | tf_op jit(solution)/shard_map/convert_element_type | solution.py:15
  72.8 3.2 %fusion.57 = (bf16[128,32,512]{2,0,1:T(8,128)(2,1)}, f32[128,32,512]{2,0,1:T(8,128)S(1)}) fusion(bf16[128,512]{1,0:T(8,128)(2,1)S(1)} %copy-done.9, bf16[128,32,128]{2,1,0:T(8,128)(2,1)S(1)} %multiply_convert_fusion.1), kind=kOutput, calls=%fused_computation.83 | convolution fusion | flops 538968064 | bytes 13762560 | tf_op jit(solution)/shard_map/while/body/eval_jaxpr/dot_general | solution.py:20
  76.5 1.8 %copy.185 = f32[128,32,128]{0,2,1:T(8,128)} copy(f32[128,32,128]{2,0,1:T(8,128)S(1)} %fusion.16) | data formatting | bytes 4194304 | tf_op jit(solution)/shard_map/while/body/eval_jaxpr/div | solution.py:25
  78.3 3.2 %fusion.52 = (bf16[128,32,128]{2,0,1:T(8,128)(2,1)S(1)}, bf16[128,32,128]{2,0,1:T(8,128)(2,1)S(1)}, bf16[128,32,128]{2,0,1:T(8,128)(2,1)}) fusion(bf16[128,32,512]{2,0,1:T(8,128)(2,1)} %get-tuple-element.66), kind=kLoop, calls=%fused_computation.78 | loop fusion | bytes 6291456 | tf_op jit(solution)/shard_map/while/body/eval_jaxpr/slice | solution.py:23
  81.5 2.3 %copy.178 = bf16[128,32,128]{0,2,1:T(8,128)(2,1)} copy(bf16[128,32,128]{2,0,1:T(8,128)(2,1)} %get-tuple-element.43) | data formatting | bytes 2097152 | tf_op jit(solution)/shard_map/while/body/eval_jaxpr/slice | solution.py:24
  83.8 1.5 %fusion.22 = bf16[4,32,128]{1,0,2:T(4,128)(2,1)S(1)} fusion(bf16[128,32,128]{2,1,0:T(8,128)(2,1)S(1)} %multiply_convert_fusion.1, bf16[4,128]{1,0:T(4,128)(2,1)S(1)} %copy-done.15), kind=kOutput, calls=%fused_computation.44 | convolution fusion | flops 4210688 | bytes 1082368 | tf_op jit(solution)/shard_map/hc,kic->hik/dot_general | solution.py:69
  85.4 7.6 %all_gather.7 = bf16[4,128,128]{2,0,1:T(4,128)(2,1)S(1)} all-gather(bf16[4,32,128]{2,0,1:T(4,128)(2,1)S(1)} %copy.181), channel_id=1, replica_groups=mesh['dp'=2,'sp'=4] {'sp'}, dimensions={1}, use_global_device_ids=true | all-gather | bytes 163840 | tf_op jit(solution)/shard_map/all_gather | solution.py:70
  93.1 1.3 copy.179
  94.4 1.3 copy.180
  95.7 8.1 %fusion.58 = (f32[32,4,128]{2,1,0:T(4,128)S(1)}, f32[32,4,128,128]{2,3,1,0:T(8,128)}) fusion(f32[4,128,128]{1,2,0:T(8,128)S(1)} %copy.183, bf16[128,32,4,32]{0,3,2,1:T(8,128)(2,1)} %bitcast.97, bf16[128,32,4,32]{0,3,2,1:T(8,128)(2,1)} %bitcast.99), kind=kOutput, calls=%fused_computation.84 | convolution fusion | flops 142606464 | bytes 10813440 | tf_op jit(solution)/shard_map/while/body/eval_jaxpr/sub | solution.py:33
  103.8 4.7 %fusion.20 = bf16[128,32,4,32]{0,3,2,1:T(8,128)(2,1)S(1)} fusion(f32[128,32,4,32]{0,3,2,1:T(8,128)S(1)} %bitcast.91, bf16[128,32,4,32]{0,3,2,1:T(8,128)(2,1)S(1)} %bitcast.94, f32[32,4,128,128]{2,3,1,0:T(8,128)} %get-tuple-element.69, f32[32,4,128]{2,1,0:T(4,128)S(1)} %get-tuple-element.68), kind=kOutput, calls=%fused_computation.31 | convolution fusion | flops 139460608 | bytes 12648448 | tf_op jit(solution)/shard_map/while/body/eval_jaxpr/jhik,kjhd->ijhd/dot_general | solution.py:34
  108.6 1.9 %fusion.51 = (f32[128,32]{0,1:T(8,128)S(1)}, f32[128,32,128]{0,2,1:T(8,128)S(1)}, f32[128,32,128]{0,2,1:T(8,128)}) fusion(f32[128,32,128]{0,2,1:T(8,128)S(1)} %copy-done.4, bf16[128,32,128]{0,2,1:T(8,128)(2,1)S(1)} %bitcast.93, bf16[128,128]{1,0:T(8,128)(2,1)S(1)} %copy-done.13), kind=kOutput, calls=%fused_computation.77 | convolution fusion | flops 135262208 | bytes 7389184 | tf_op jit(solution)/shard_map/while/body/eval_jaxpr/dot_general | solution.py:37
  111.5 4.2 %add_convert_fusion = bf16[128,32,128]{0,2,1:T(8,128)(2,1)S(1)} fusion(f32[128,32,128]{0,2,1:T(8,128)} %get-tuple-element.70, f32[128,32,128]{0,2,1:T(8,128)S(1)} %get-tuple-element.31, f32[128,32]{0,1:T(8,128)S(1)} %add_rsqrt_fusion, f32[128,32]{0,1:T(8,128)S(1)} %broadcast_multiply_fusion, bf16[512,128]{1,0:T(8,128)(2,1)S(1)} %copy-done.10, ...), kind=kOutput, calls=%fused_computation.35 | convolution fusion | flops 1080557568 | bytes 5537792 | tf_op jit(solution)/shard_map/while/body/eval_jaxpr/dot_general | solution.py:42
  116.6 17.1 %all_to_all.9 = bf16[128,32,128]{2,1,0:T(8,128)(2,1)S(1)} all-to-all(bf16[128,32,128]{2,1,0:T(8,128)(2,1)S(1)} %copy.191), channel_id=1, replica_groups=mesh['dp'=2,'sp'=4] {'sp'}, dimensions={0} | all-to-all | bytes 2097152 | tf_op jit(solution)/shard_map/all_to_all | solution.py:82
  134.3 1.4 copy-done.3
  135.6 1.6 %bitcast_add_fusion = f32[32,128,128]{2,1,0:T(8,128)} fusion(f32[32,128,128]{2,1,0:T(8,128)S(1)} %copy-done.3, f32[32,4,32,128]{3,2,1,0:T(8,128)S(1)} %copy.192), kind=kLoop, calls=%fused_computation.29 | loop fusion | flops 524288 | bytes 6291456 | tf_op jit(solution)/shard_map/add | solution.py:83
  (53 shorter events, 7.5 us)
Async XLA Ops:
  0.0 3.7 %copy-start = (bf16[128,512]{1,0:T(8,128)(2,1)S(1)}, bf16[128,512]{1,0:T(8,128)(2,1)}, u32[]{:S(2)}) copy-start(bf16[128,512]{1,0:T(8,128)(2,1)} %param.10) | copy-start | bytes 393220
  0.0 2.4 %copy-start.2 = (f32[32,128,128]{2,1,0:T(8,128)S(1)}, f32[32,128,128]{2,1,0:T(8,128)}, u32[]{:S(2)}) copy-start(f32[32,128,128]{2,1,0:T(8,128)} %param.9) | copy-start | bytes 6291460
  15.5 2.3 %copy-start.14 = (bf16[4,128]{1,0:T(4,128)(2,1)S(1)}, bf16[4,128]{1,0:T(4,128)(2,1)}, u32[]{:S(2)}) copy-start(bf16[4,128]{1,0:T(4,128)(2,1)} %param.11) | copy-start | bytes 3076
  30.4 3.6 %copy-start.8 = (f32[4,128,128]{1,2,0:T(8,128)S(1)}, f32[4,128,128]{1,2,0:T(8,128)}, u32[]{:S(2)}) copy-start(f32[4,128,128]{1,2,0:T(8,128)} %copy.163) | copy-start | bytes 786436
  34.0 8.0 %copy-start.7 = (bf16[32,128,128]{1,2,0:T(8,128)(2,1)S(1)}, bf16[32,128,128]{1,2,0:T(8,128)(2,1)}, u32[]{:S(2)}) copy-start(bf16[32,128,128]{1,2,0:T(8,128)(2,1)} %copy.159) | copy-start | bytes 3145732
  42.0 5.2 %copy-start.12 = (bf16[128,128]{1,0:T(8,128)(2,1)S(1)}, bf16[128,128]{1,0:T(8,128)(2,1)}, u32[]{:S(2)}) copy-start(bf16[128,128]{1,0:T(8,128)(2,1)} %param.12) | copy-start | bytes 98308
  69.9 2.9 %copy-start.9 = (bf16[128,512]{1,0:T(8,128)(2,1)S(1)}, bf16[128,512]{1,0:T(8,128)(2,1)}, u32[]{:S(2)}) copy-start(bf16[128,512]{1,0:T(8,128)(2,1)} %param.13) | copy-start | bytes 393220
  81.5 2.3 %copy-start.15 = (bf16[4,128]{1,0:T(4,128)(2,1)S(1)}, bf16[4,128]{1,0:T(4,128)(2,1)}, u32[]{:S(2)}) copy-start(bf16[4,128]{1,0:T(4,128)(2,1)} %param.14) | copy-start | bytes 3076
  95.7 8.1 %copy-start.5 = (f32[128,32,128]{0,2,1:T(8,128)S(1)}, f32[128,32,128]{0,2,1:T(8,128)}, u32[]{:S(2)}) copy-start(f32[128,32,128]{0,2,1:T(8,128)} %copy.185) | copy-start | bytes 6291460
  95.7 8.1 %copy-start.6 = (bf16[128,32,128]{0,2,1:T(8,128)(2,1)S(1)}, bf16[128,32,128]{0,2,1:T(8,128)(2,1)}, u32[]{:S(2)}) copy-start(bf16[128,32,128]{0,2,1:T(8,128)(2,1)} %copy.178) | copy-start | bytes 3145732
  103.8 4.8 %copy-start.4 = (f32[128,32,128]{0,2,1:T(8,128)S(1)}, f32[128,32,128]{0,2,1:T(8,128)}, u32[]{:S(2)}) copy-start(f32[128,32,128]{0,2,1:T(8,128)} %copy.188) | copy-start | bytes 6291460
  103.8 4.8 %copy-start.13 = (bf16[128,128]{1,0:T(8,128)(2,1)S(1)}, bf16[128,128]{1,0:T(8,128)(2,1)}, u32[]{:S(2)}) copy-start(bf16[128,128]{1,0:T(8,128)(2,1)} %param.15) | copy-start | bytes 98308
  110.5 0.9 copy-start.10
  110.5 1.0 copy-start.11
  134.0 1.6 %copy-start.3 = (f32[32,128,128]{2,1,0:T(8,128)S(1)}, f32[32,128,128]{2,1,0:T(8,128)}, u32[]{:S(2)}) copy-start(f32[32,128,128]{2,1,0:T(8,128)} %get-tuple-element.65) | copy-start | bytes 6291460
  134.2 3.0 %copy-start.1 = (bf16[128,512]{1,0:T(8,128)(2,1)S(1)}, bf16[128,512]{1,0:T(8,128)(2,1)}, u32[]{:S(2)}) copy-start(bf16[128,512]{1,0:T(8,128)(2,1)} %param.10) | copy-start | bytes 393220
where the time goes:
time: 138 us; the launch traced here: 137 us
  blocking collectives  51.8 us (38%)
  matrix products  43.3 us (31%)
  local copies, waits for them, and re-layouts  29.5 us (21%)
  other arithmetic  12.3 us (9%)
    all_to_all x1, blocking collectives, local_fn(): delta_rows = lax.all_to_all(delta_cols, 'sp', 0, 1, tiled=True)  17.1 us
    all_to_all x1, blocking collectives, local_fn(): lax.all_to_all(pair_one.astype(jnp.bfloat16), 'sp', 1, 0, tiled=True)  16.9 us
    sub x2, matrix products, attend(): attn_prob = jax.nn.softmax(scores, axis=-1).astype(jnp.bfloat16)  16.1 us
    all_gather x1, blocking collectives, local_fn(): bias_s = lax.all_gather(bias_loc, 'sp', axis=1, tiled=True)  10.3 us
    dot_general x2, matrix products, attend(): jnp.einsum(mix_form, attn_prob, val_vecs, preferred_element_type=jnp.floa...  9.94 us
    slice x4, local copies, waits for them, and re-layouts, project(): projected[..., channels:2 * channels].astype(jnp.bfloat16)  9.33 us
    all_gather x1, blocking collectives, local_fn(): bias_e = lax.all_gather(bias_loc_e, 'sp', axis=1, tiled=True)  7.56 us
    dot_general x2, matrix products, project(): projected = jnp.dot(normed, w_qkvg, preferred_element_type=jnp.float32)  6.57 us

commit v1 on v0

v1 whole, which is shorter than its diff:
```python
import functools

import jax
import jax.numpy as jnp
from jax import lax
from jax.experimental import pallas as pl
from jax.experimental.pallas import tpu as pltpu
from jax.sharding import PartitionSpec as P

MESH = pl.DeviceIdType.MESH
EPS = 1e-5
LOG2E = 1.4426950408889634
BF = jnp.bfloat16
F32 = jnp.float32


def dot(a, b):
    return jnp.dot(a, b, preferred_element_type=F32)


def dot_tn(a, b):
    return lax.dot_general(a, b, (((0,), (0,)), ((), ())), preferred_element_type=F32)


def norm_t(xt):
    mean = jnp.sum(xt, axis=0, keepdims=True) * (1.0 / xt.shape[0])
    cen = xt - mean
    var = jnp.sum(cen * cen, axis=0, keepdims=True) * (1.0 / xt.shape[0])
    return (cen * lax.rsqrt(var + EPS)).astype(BF)


def sigmoid(x):
    return 0.5 * jnp.tanh(0.5 * x) + 0.5


def attend(kn, qt, vt, bias_ref, heads):
    hd, n = qt.shape
    d = hd // heads
    scale = LOG2E * d ** -0.5
    outs = []
    for pair in range(heads // 2):
        cols = []
        for h in (2 * pair, 2 * pair + 1):
            parts = []
            if h:
                parts.append(jnp.zeros((h * d, n), BF))
            parts.append(qt[h * d:(h + 1) * d])
            if h < heads - 1:
                parts.append(jnp.zeros(((heads - 1 - h) * d, n), BF))
            cols.append(jnp.concatenate(parts, axis=0))
        s = dot(kn, jnp.concatenate(cols, axis=1)) * scale + bias_ref[:, 2 * pair * n:(2 * pair + 2) * n]
        e = jnp.exp2(s - jnp.max(s, axis=0, keepdims=True))
        p = (e * (1.0 / jnp.sum(e, axis=0, keepdims=True))).astype(BF)
        o = dot(vt[2 * pair * d:(2 * pair + 2) * d], p)
        outs += [o[:d, :n], o[d:, n:]]
    return jnp.concatenate(outs, axis=0)


def project(wt, ut, n, qv_ref, kn_ref, g_ref, p):
    c = ut.shape[0]
    qv_ref[p, :c] = dot(wt[0:c], ut).astype(BF)
    kt = dot(wt[c:2 * c], ut).astype(BF)
    kn_ref[2 * p] = kt[:, :n].T
    kn_ref[2 * p + 1] = kt[:, n:].T
    qv_ref[p, c:] = dot(wt[2 * c:3 * c], ut).astype(BF)
    g_ref[p] = sigmoid(dot(wt[3 * c:], ut))


def kernel(z_hbm, wqs, wbs, wos, wqe, wbe, woe, w1, w2, y_hbm,
           z, ut, qv, kn, g, bloc, bsend, ball, biast, hsend, hcol, besend, beall, dsend, drecv, y,
           wqst, wqet, woet, w1t, w2t,
           zsem, ysem, bs_s, bs_r, h_s, h_r, be_s, be_r, d_s, d_r):
    rows, n, c = z.shape
    heads = wbs.shape[0]
    dp, sp = lax.axis_index("dp"), lax.axis_index("sp")
    x, core = sp // 2, sp % 2
    peers = [2 * (1 - x) + core, 2 * (1 - x) + 1 - core, 2 * x + 1 - core]
    mine = pl.multiple_of(sp * rows, rows)
    zchunks = 4
    zr = rows // zchunks

    def zcopy(i):
        return pltpu.make_async_copy(z_hbm.at[pl.ds(i * zr, zr)], z.at[pl.ds(i * zr, zr)], zsem.at[i])

    for i in range(zchunks):
        zcopy(i).start()
    bar = pltpu.get_barrier_semaphore()
    for t in peers:
        pl.semaphore_signal(bar, inc=1, device_id=(dp, t), device_id_type=MESH)

    def remote(src, dst, ssem, rsem, t):
        return pltpu.make_async_remote_copy(src, dst, ssem, rsem, device_id=(dp, t), device_id_type=MESH)

    wqst[...] = wqs[...].T
    wqet[...] = wqe[...].T
    woet[...] = woe[...].T
    w1t[...] = w1[...].T
    w2t[...] = w2[...].T

    for i in range(zchunks):
        zcopy(i).wait()

        def ln_pair(p, _):
            u = norm_t(jnp.concatenate([z[2 * p].T, z[2 * p + 1].T], axis=1))
            ut[p] = u
            b = dot(wbs[...], u)
            bloc[:, 2 * p] = b[:, :n]
            bloc[:, 2 * p + 1] = b[:, n:]
            return _
        lax.fori_loop(i * zr // 2, (i + 1) * zr // 2, ln_pair, 0)
    bsend[...] = bloc[...].astype(BF)
    ball[:, pl.ds(mine, rows)] = bsend[...]
    pl.semaphore_wait(bar, 3)
    bias_sends = []
    for k, t in enumerate(peers):
        cp = remote(bsend, ball.at[:, pl.ds(mine, rows)], bs_s.at[k], bs_r.at[sp], t)
        cp.start()
        bias_sends.append(cp)

    def proj_pair(p, _):
        project(wqst, ut[p], n, qv, kn, g, p)
        return _
    lax.fori_loop(0, rows // 2, proj_pair, 0)
    for k, t in enumerate(peers):
        remote(bsend, ball.at[:, pl.ds(pl.multiple_of(t * rows, rows), rows)], bs_s.at[k], bs_r.at[t], t).wait_recv()
    for h in range(heads):
        biast[:, h * n:(h + 1) * n] = ball[h].astype(F32).T * LOG2E

    def start_pair(p, _):
        ogs = []
        for r in range(2):
            o = attend(kn[2 * p + r], qv[p, :c, r * n:(r + 1) * n], qv[p, c:, r * n:(r + 1) * n], biast, heads)
            ogs.append((o * g[p, :, r * n:(r + 1) * n]).astype(BF))
        upd = dot_tn(jnp.concatenate(ogs, axis=1), wos[...])
        uts = []
        for r in range(2):
            z1 = z[2 * p + r] + upd[r * n:(r + 1) * n]
            z[2 * p + r] = z1
            uts.append(z1.astype(BF).astype(F32).T)
        b = dot(wbe[...], norm_t(jnp.concatenate(uts, axis=1)))
        bloc[:, 2 * p] = b[:, :n]
        bloc[:, 2 * p + 1] = b[:, n:]
        return _

    groups = rows // 16
    chunks = 4
    cols = rows // chunks
    h_sends = []
    for gi in range(groups):
        lax.fori_loop(gi * 8, (gi + 1) * 8, start_pair, 0)

        def shuffle(jb, _):
            j0 = pl.multiple_of(jb * 8, 8)
            blk = jnp.swapaxes(z[gi * 16:(gi + 1) * 16, pl.ds(j0, 8)], 0, 1)
            hsend[pl.ds(j0, 8), gi * 16:(gi + 1) * 16] = blk.astype(BF)
            return _
        lax.fori_loop(0, n // 8, shuffle, 0)
        dst_rows = pl.ds(pl.multiple_of(mine + gi * 16, 16), 16)
        for ch in range(chunks):
            for k, t in enumerate(peers):
                cp = remote(hsend.at[pl.ds(t * rows + ch * cols, cols), gi * 16:(gi + 1) * 16],
                            hcol.at[ch * cols:(ch + 1) * cols, dst_rows],
                            h_s.at[gi, ch, k], h_r.at[gi, ch, sp], t)
                cp.start()
                h_sends.append(cp)
        hcol[:, dst_rows] = hsend[pl.ds(mine, rows), gi * 16:(gi + 1) * 16]
    besend[...] = bloc[...].astype(BF)
    beall[:, pl.ds(mine, rows)] = besend[...]
    for k, t in enumerate(peers):
        cp = remote(besend, beall.at[:, pl.ds(mine, rows)], be_s.at[k], be_r.at[sp], t)
        cp.start()
        bias_sends.append(cp)
    for k, t in enumerate(peers):
        remote(besend, beall.at[:, pl.ds(pl.multiple_of(t * rows, rows), rows)], be_s.at[k], be_r.at[t], t).wait_recv()
    for h in range(heads):
        biast[:, h * n:(h + 1) * n] = beall[h].astype(F32) * LOG2E

    def end_pair(p, _):
        wt = jnp.concatenate([hcol[2 * p].astype(F32).T, hcol[2 * p + 1].astype(F32).T], axis=1)
        project(wqet, norm_t(wt), n, qv, kn, g, p)
        ogs = []
        for r in range(2):
            o = attend(kn[2 * p + r], qv[p, :c, r * n:(r + 1) * n], qv[p, c:, r * n:(r + 1) * n], biast, heads)
            ogs.append((o * g[p, :, r * n:(r + 1) * n]).astype(BF))
        e = dot(woet[...], jnp.concatenate(ogs, axis=1))
        hid = jnp.maximum(dot(w1t[...], norm_t(wt + e)), 0.0).astype(BF)
        delta = (e + dot(w2t[...], hid)).astype(BF)
        dsend[2 * p] = delta[:, :n].T
        dsend[2 * p + 1] = delta[:, n:].T
        return _

    d_sends = []
    for ch in range(chunks):
        for gi in range(groups):
            for k, t in enumerate(peers):
                remote(hsend.at[pl.ds(t * rows + ch * cols, cols), gi * 16:(gi + 1) * 16],
                       hcol.at[ch * cols:(ch + 1) * cols, pl.ds(pl.multiple_of(t * rows + gi * 16, 16), 16)],
                       h_s.at[gi, ch, k], h_r.at[gi, ch, t], t).wait_recv()
        lax.fori_loop(ch * cols // 2, (ch + 1) * cols // 2, end_pair, 0)
        for k, t in enumerate(peers):
            cp = remote(dsend.at[ch * cols:(ch + 1) * cols, pl.ds(pl.multiple_of(t * rows, rows), rows)],
                        drecv.at[pl.ds(mine + ch * cols, cols)],
                        d_s.at[ch, k], d_r.at[ch, sp], t)
            cp.start()
            d_sends.append(cp)
    drecv[pl.ds(mine, rows)] = dsend[:, pl.ds(mine, rows)]

    def final_block(j0):
        for gi in range(groups):
            blk = jnp.swapaxes(drecv[pl.ds(j0, 8), gi * 16:(gi + 1) * 16].astype(F32), 0, 1)
            y[gi * 16:(gi + 1) * 16, pl.ds(j0, 8)] = z[gi * 16:(gi + 1) * 16, pl.ds(j0, 8)] + blk

    for ch in range(chunks):
        final_block(pl.multiple_of(mine + ch * cols, 8))
    for ch in range(chunks):
        for k, t in enumerate(peers):
            remote(dsend.at[ch * cols:(ch + 1) * cols, pl.ds(pl.multiple_of(t * rows, rows), rows)],
                   drecv.at[pl.ds(t * rows + ch * cols, cols)],
                   d_s.at[ch, k], d_r.at[ch, t], t).wait_recv()
            final_block(pl.multiple_of(t * rows + ch * cols, 8))
    ycopy = pltpu.make_async_copy(y, y_hbm, ysem)
    ycopy.start()
    for cp in bias_sends + h_sends + d_sends:
        cp.wait_send()
    ycopy.wait()


def solution(mesh):
    row_spec = P(('dp', 'sp'), None, None)
    sp = mesh.shape['sp']

    def local_fn(pair_loc, wqs, wbs, wos, wqe, wbe, woe, w1, w2):
        rows, n, c = pair_loc.shape
        heads = wbs.shape[0]
        dma = pltpu.SemaphoreType.DMA
        vmem = pl.BlockSpec(memory_space=pltpu.VMEM)
        return pl.pallas_call(
            kernel,
            out_shape=jax.ShapeDtypeStruct(pair_loc.shape, F32),
            in_specs=[pl.BlockSpec(memory_space=pl.ANY)] + [vmem] * 8,
            out_specs=pl.BlockSpec(memory_space=pl.ANY),
            scratch_shapes=[
                pltpu.VMEM((rows, n, c), F32),
                pltpu.VMEM((rows // 2, c, 2 * n), BF),
                pltpu.VMEM((rows // 2, 2 * c, 2 * n), BF),
                pltpu.VMEM((rows, n, c), BF),
                pltpu.VMEM((rows // 2, c, 2 * n), F32),
                pltpu.VMEM((heads, rows, n), F32),
                pltpu.VMEM((heads, rows, n), BF),
                pltpu.VMEM((heads, n, n), BF),
                pltpu.VMEM((n, heads * n), F32),
                pltpu.VMEM((n, rows, c), BF),
                pltpu.VMEM((rows, n, c), BF),
                pltpu.VMEM((heads, rows, n), BF),
                pltpu.VMEM((heads, n, n), BF),
                pltpu.VMEM((rows, n, c), BF),
                pltpu.VMEM((n, rows, c), BF),
                pltpu.VMEM((rows, n, c), F32),
                pltpu.VMEM(wqs.shape[::-1], BF),
                pltpu.VMEM(wqe.shape[::-1], BF),
                pltpu.VMEM(woe.shape[::-1], BF),
                pltpu.VMEM(w1.shape[::-1], BF),
                pltpu.VMEM(w2.shape[::-1], BF),
                dma((4,)), dma,
                dma((3,)), dma((sp,)),
                dma((rows // 16, 4, 3)), dma((rows // 16, 4, sp)),
                dma((3,)), dma((sp,)),
                dma((4, 3)), dma((4, sp)),
            ],
            compiler_params=pltpu.CompilerParams(collective_id=0, has_side_effects=True, vmem_limit_bytes=60 * 2 ** 20),
            name="pair_block",
        )(pair_loc, wqs, wbs, wos, wqe, wbe, woe, w1, w2)

    return jax.shard_map(local_fn, mesh=mesh, in_specs=(row_spec,) + (P(),) * 8, out_specs=row_spec, check_vma=False)
```

time: 138 us -> 88.9 us (0.64)
  Pallas kernels: 0 us -> 85.6 us
  blocking collectives: 51.8 us -> 0 us
  matrix products: 43.3 us -> 0 us
  local copies, waits for them, and re-layouts: 29.5 us -> 3.14 us
  other arithmetic: 12.3 us -> 0 us
    pallas_call x0 -> x1, Pallas kernels: none -> 85.6 us  [local_fn(): pl.pallas_call(kernel, out_shape=jax.ShapeDtypeStruct(pair_loc.shape, F32...]
    all_to_all x2 -> x0, blocking collectives: 34 us -> none  [the longest x1 17.1 us: local_fn(): delta_rows = lax.all_to_all(delta_cols, 'sp', 0, 1, tiled=True)]
    dot_general x9 -> x0, matrix products: 27.3 us -> none  [the longest x2 9.94 us: attend(): jnp.einsum(mix_form, attn_prob, val_vecs, preferred_element_type=jnp.floa...]
    all_gather x2 -> x0, blocking collectives: 17.8 us -> none  [the longest x1 10.3 us: local_fn(): bias_s = lax.all_gather(bias_loc, 'sp', axis=1, tiled=True)]
    slice x8 -> x0, local copies, waits for them, and re-layouts: 17.6 us -> none  [the longest x4 9.33 us: project(): projected[..., channels:2 * channels].astype(jnp.bfloat16)]
    sub x2 -> x0, matrix products: 16.1 us -> none  [attend(): attn_prob = jax.nn.softmax(scores, axis=-1).astype(jnp.bfloat16)]
    reduce_sum x5 -> x0, other arithmetic: 5.95 us -> none  [the longest x2 3.02 us: layer_norm(): mean_c = jnp.mean(vals_f, axis=-1, keepdims=True)]
    convert_element_type x8 -> x0, local copies, waits for them, and re-layouts: 5.05 us -> none  [the longest x2 2.12 us: layer_norm(): vals_f = values.astype(jnp.float32)]
where the time goes in v1:
time: 88.9 us; the launch traced here: 88.8 us
  Pallas kernels  85.6 us (96%)
  local copies, waits for them, and re-layouts  3.14 us (4%)
    pallas_call x1, Pallas kernels, local_fn(): pl.pallas_call(kernel, out_shape=jax.ShapeDtypeStruct(pair_loc.shape, F32...  85.6 us
    unnamed x1, local copies, waits for them, and re-layouts  3.14 us

profile of v1, /device:TPU:0, one launch (start us, length us, event | category | flops | bytes accessed | tf_op | source)
XLA Modules:
  0.0 88.8 jit_solution(1830188349761732635)
XLA Ops:
  0.0 85.6 %pair_block.1 = f32[32,128,128]{2,1,0:T(8,128)} custom-call(f32[32,128,128]{2,1,0:T(8,128)} %z_hbm.1, bf16[128,512]{1,0:T(8,128)(2,1)} %wqs.1, bf16[4,128]{1,0:T(4,128)(2,1)} %wbs.1, bf16[128,128]{1,0:T(8,128)(2,1)} %wos.1, bf16[128,512]{1,0:T(8,128)(2,1)} %wqe.1, bf16[4,128]{1,0:T(4,128)(2,1)} %wbe.1, bf16[128,128]{1,0:T(8,128)(2,1)} %woe.1, ...), custom_call_target="tpu_custom_call" | custom-call | tf_op jit(solution)/shard_map/pair_block/pallas_call | solution.py:237
  85.6 3.1 %copy.11 = f32[32,128,128]{2,1,0:T(8,128)} copy(f32[32,128,128]{2,1,0:T(8,128)} %pair_block.1) | data formatting | bytes 4194304

commit v2 on v1

--- a/solution.py
+++ b/solution.py
@@ -33,41 +33,62 @@
     return 0.5 * jnp.tanh(0.5 * x) + 0.5
 
 
-def attend(kn, qt, vt, bias_ref, heads):
+def block_diag(qt, pair, heads):
     hd, n = qt.shape
     d = hd // heads
+    cols = []
+    for h in (2 * pair, 2 * pair + 1):
+        parts = []
+        if h:
+            parts.append(jnp.zeros((h * d, n), BF))
+        parts.append(qt[h * d:(h + 1) * d])
+        if h < heads - 1:
+            parts.append(jnp.zeros(((heads - 1 - h) * d, n), BF))
+        cols.append(jnp.concatenate(parts, axis=0))
+    return jnp.concatenate(cols, axis=1)
+
+
+def stage_scores(kn, qv, s, p, heads):
+    c, n = kn.shape[1:]
+    for r in range(2):
+        keys = kn[2 * p + r]
+        qt = qv[p, :c, r * n:(r + 1) * n]
+        for pair in range(heads // 2):
+            s[r, :, 2 * pair * n:(2 * pair + 2) * n] = dot(keys, block_diag(qt, pair, heads))
+
+
+def stage_mix(s, biast, qv, g, og, p, heads):
+    n = s.shape[1]
+    c = qv.shape[1] // 2
+    d = c // heads
     scale = LOG2E * d ** -0.5
-    outs = []
-    for pair in range(heads // 2):
-        cols = []
-        for h in (2 * pair, 2 * pair + 1):
-            parts = []
-            if h:
-                parts.append(jnp.zeros((h * d, n), BF))
-            parts.append(qt[h * d:(h + 1) * d])
-            if h < heads - 1:
-                parts.append(jnp.zeros(((heads - 1 - h) * d, n), BF))
-            cols.append(jnp.concatenate(parts, axis=0))
-        s = dot(kn, jnp.concatenate(cols, axis=1)) * scale + bias_ref[:, 2 * pair * n:(2 * pair + 2) * n]
-        e = jnp.exp2(s - jnp.max(s, axis=0, keepdims=True))
-        p = (e * (1.0 / jnp.sum(e, axis=0, keepdims=True))).astype(BF)
-        o = dot(vt[2 * pair * d:(2 * pair + 2) * d], p)
-        outs += [o[:d, :n], o[d:, n:]]
-    return jnp.concatenate(outs, axis=0)
-
-
-def project(wt, ut, n, qv_ref, kn_ref, g_ref, p):
-    c = ut.shape[0]
-    qv_ref[p, :c] = dot(wt[0:c], ut).astype(BF)
-    kt = dot(wt[c:2 * c], ut).astype(BF)
+    for r in range(2):
+        for pair in range(heads // 2):
+            probs = []
+            for h in (2 * pair, 2 * pair + 1):
+                t = s[r, :, h * n:(h + 1) * n] * scale + biast[:, h * n:(h + 1) * n]
+                e = jnp.exp2(t - jnp.max(t, axis=0, keepdims=True))
+                probs.append((e * (1.0 / jnp.sum(e, axis=0, keepdims=True))).astype(BF))
+            rows = slice(c + 2 * pair * d, c + (2 * pair + 2) * d)
+            o = dot(qv[p, rows, r * n:(r + 1) * n], jnp.concatenate(probs, axis=1))
+            for i in range(2):
+                h = 2 * pair + i
+                out = o[i * d:(i + 1) * d, i * n:(i + 1) * n] * g[p, h * d:(h + 1) * d, r * n:(r + 1) * n]
+                og[p, h * d:(h + 1) * d, r * n:(r + 1) * n] = out.astype(BF)
+
+
+def project(wt, u, n, qv_ref, kn_ref, g_ref, p):
+    c = u.shape[0]
+    qv_ref[p, :c] = dot(wt[0:c], u).astype(BF)
+    kt = dot(wt[c:2 * c], u).astype(BF)
     kn_ref[2 * p] = kt[:, :n].T
     kn_ref[2 * p + 1] = kt[:, n:].T
-    qv_ref[p, c:] = dot(wt[2 * c:3 * c], ut).astype(BF)
-    g_ref[p] = sigmoid(dot(wt[3 * c:], ut))
+    qv_ref[p, c:] = dot(wt[2 * c:3 * c], u).astype(BF)
+    g_ref[p] = sigmoid(dot(wt[3 * c:], u))
 
 
 def kernel(z_hbm, wqs, wbs, wos, wqe, wbe, woe, w1, w2, y_hbm,
-           z, ut, qv, kn, g, bloc, bsend, ball, biast, hsend, hcol, besend, beall, dsend, drecv, y,
+           z, ut, qv, kn, g, bloc, bsend, ball, biast, hsend, hcol, besend, beall, dsend, drecv, y, s, og, eb, u2,
            wqst, wqet, woet, w1t, w2t,
            zsem, ysem, bs_s, bs_r, h_s, h_r, be_s, be_r, d_s, d_r):
     rows, n, c = z.shape
@@ -126,20 +147,23 @@
     for h in range(heads):
         biast[:, h * n:(h + 1) * n] = ball[h].astype(F32).T * LOG2E
 
-    def start_pair(p, _):
-        ogs = []
-        for r in range(2):
-            o = attend(kn[2 * p + r], qv[p, :c, r * n:(r + 1) * n], qv[p, c:, r * n:(r + 1) * n], biast, heads)
-            ogs.append((o * g[p, :, r * n:(r + 1) * n]).astype(BF))
-        upd = dot_tn(jnp.concatenate(ogs, axis=1), wos[...])
-        uts = []
-        for r in range(2):
-            z1 = z[2 * p + r] + upd[r * n:(r + 1) * n]
-            z[2 * p + r] = z1
-            uts.append(z1.astype(BF).astype(F32).T)
-        b = dot(wbe[...], norm_t(jnp.concatenate(uts, axis=1)))
+    last = rows // 2 - 1
+
+    def lag(t, by):
+        return jnp.clip(t - by, 0, last)
+
+    def start_step(t, _):
+        p = lag(t, 3)
+        u = norm_t(jnp.concatenate([y[2 * p].astype(BF).astype(F32).T, y[2 * p + 1].astype(BF).astype(F32).T], axis=1))
+        b = dot(wbe[...], u)
         bloc[:, 2 * p] = b[:, :n]
         bloc[:, 2 * p + 1] = b[:, n:]
+        p = lag(t, 2)
+        upd = dot_tn(og[p], wos[...])
+        y[2 * p] = z[2 * p] + upd[:n]
+        y[2 * p + 1] = z[2 * p + 1] + upd[n:]
+        stage_mix(s, biast, qv, g, og, lag(t, 1), heads)
+        stage_scores(kn, qv, s, lag(t, 0), heads)
         return _
 
     groups = rows // 16
@@ -147,11 +171,11 @@
     cols = rows // chunks
     h_sends = []
     for gi in range(groups):
-        lax.fori_loop(gi * 8, (gi + 1) * 8, start_pair, 0)
+        lax.fori_loop(gi * 8 + 2 * (gi > 0), (gi + 1) * 8 + 2 + (gi == groups - 1), start_step, 0)
 
         def shuffle(jb, _):
             j0 = pl.multiple_of(jb * 8, 8)
-            blk = jnp.swapaxes(z[gi * 16:(gi + 1) * 16, pl.ds(j0, 8)], 0, 1)
+            blk = jnp.swapaxes(y[gi * 16:(gi + 1) * 16, pl.ds(j0, 8)], 0, 1)
             hsend[pl.ds(j0, 8), gi * 16:(gi + 1) * 16] = blk.astype(BF)
             return _
         lax.fori_loop(0, n // 8, shuffle, 0)
@@ -175,40 +199,47 @@
     for h in range(heads):
         biast[:, h * n:(h + 1) * n] = beall[h].astype(F32) * LOG2E
 
-    def end_pair(p, _):
+    def end_step(t, _):
+        p = lag(t, 4)
+        hid = jnp.maximum(dot(w1t[...], u2[p % 2]), 0.0).astype(BF)
+        delta = (eb[p % 2] + dot(w2t[...], hid)).astype(BF)
+        dsend[2 * p] = delta[:, :n].T
+        dsend[2 * p + 1] = delta[:, n:].T
+        p = lag(t, 3)
+        wt = jnp.concatenate([hcol[2 * p].astype(F32).T, hcol[2 * p + 1].astype(F32).T], axis=1)
+        e = dot(woet[...], og[p])
+        eb[p % 2] = e
+        u2[p % 2] = norm_t(wt + e)
+        stage_mix(s, biast, qv, g, og, lag(t, 2), heads)
+        stage_scores(kn, qv, s, lag(t, 1), heads)
+        p = lag(t, 0)
         wt = jnp.concatenate([hcol[2 * p].astype(F32).T, hcol[2 * p + 1].astype(F32).T], axis=1)
         project(wqet, norm_t(wt), n, qv, kn, g, p)
-        ogs = []
-        for r in range(2):
-            o = attend(kn[2 * p + r], qv[p, :c, r * n:(r + 1) * n], qv[p, c:, r * n:(r + 1) * n], biast, heads)
-            ogs.append((o * g[p, :, r * n:(r + 1) * n]).astype(BF))
-        e = dot(woet[...], jnp.concatenate(ogs, axis=1))
-        hid = jnp.maximum(dot(w1t[...], norm_t(wt + e)), 0.0).astype(BF)
-        delta = (e + dot(w2t[...], hid)).astype(BF)
-        dsend[2 * p] = delta[:, :n].T
-        dsend[2 * p + 1] = delta[:, n:].T
         return _
 
     d_sends = []
-    for ch in range(chunks):
-        for gi in range(groups):
+    per = cols // 2
+    for ch in range(chunks + 1):
+        if ch < chunks:
+            for gi in range(groups):
+                for k, t in enumerate(peers):
+                    remote(hsend.at[pl.ds(t * rows + ch * cols, cols), gi * 16:(gi + 1) * 16],
+                           hcol.at[ch * cols:(ch + 1) * cols, pl.ds(pl.multiple_of(t * rows + gi * 16, 16), 16)],
+                           h_s.at[gi, ch, k], h_r.at[gi, ch, t], t).wait_recv()
+        lax.fori_loop(ch * per, (ch + 1) * per, end_step, 0)
+        if ch:
             for k, t in enumerate(peers):
-                remote(hsend.at[pl.ds(t * rows + ch * cols, cols), gi * 16:(gi + 1) * 16],
-                       hcol.at[ch * cols:(ch + 1) * cols, pl.ds(pl.multiple_of(t * rows + gi * 16, 16), 16)],
-                       h_s.at[gi, ch, k], h_r.at[gi, ch, t], t).wait_recv()
-        lax.fori_loop(ch * cols // 2, (ch + 1) * cols // 2, end_pair, 0)
-        for k, t in enumerate(peers):
-            cp = remote(dsend.at[ch * cols:(ch + 1) * cols, pl.ds(pl.multiple_of(t * rows, rows), rows)],
-                        drecv.at[pl.ds(mine + ch * cols, cols)],
-                        d_s.at[ch, k], d_r.at[ch, sp], t)
-            cp.start()
-            d_sends.append(cp)
+                cp = remote(dsend.at[(ch - 1) * cols:ch * cols, pl.ds(pl.multiple_of(t * rows, rows), rows)],
+                            drecv.at[pl.ds(mine + (ch - 1) * cols, cols)],
+                            d_s.at[ch - 1, k], d_r.at[ch - 1, sp], t)
+                cp.start()
+                d_sends.append(cp)
     drecv[pl.ds(mine, rows)] = dsend[:, pl.ds(mine, rows)]
 
     def final_block(j0):
         for gi in range(groups):
             blk = jnp.swapaxes(drecv[pl.ds(j0, 8), gi * 16:(gi + 1) * 16].astype(F32), 0, 1)
-            y[gi * 16:(gi + 1) * 16, pl.ds(j0, 8)] = z[gi * 16:(gi + 1) * 16, pl.ds(j0, 8)] + blk
+            y[gi * 16:(gi + 1) * 16, pl.ds(j0, 8)] += blk
 
     for ch in range(chunks):
         final_block(pl.multiple_of(mine + ch * cols, 8))
@@ -256,6 +287,10 @@
                 pltpu.VMEM((rows, n, c), BF),
                 pltpu.VMEM((n, rows, c), BF),
                 pltpu.VMEM((rows, n, c), F32),
+                pltpu.VMEM((2, n, heads * n), F32),
+                pltpu.VMEM((rows // 2, c, 2 * n), BF),
+                pltpu.VMEM((2, c, 2 * n), F32),
+                pltpu.VMEM((2, c, 2 * n), BF),
                 pltpu.VMEM(wqs.shape[::-1], BF),
                 pltpu.VMEM(wqe.shape[::-1], BF),
                 pltpu.VMEM(woe.shape[::-1], BF),

time: 88.9 us -> 55.8 us (0.63)
  Pallas kernels: 85.6 us -> 52.5 us
    pallas_call x1, Pallas kernels: 85.6 us -> 52.5 us  [local_fn(): pl.pallas_call(kernel, out_shape=jax.ShapeDtypeStruct(pair_loc.shape, F32...]
where the time goes in v2:
time: 55.8 us; the launch traced here: 55.7 us
  Pallas kernels  52.5 us (94%)
  local copies, waits for them, and re-layouts  3.14 us (6%)
    pallas_call x1, Pallas kernels, local_fn(): pl.pallas_call(kernel, out_shape=jax.ShapeDtypeStruct(pair_loc.shape, F32...  52.5 us
    unnamed x1, local copies, waits for them, and re-layouts  3.14 us

profile of v2, /device:TPU:0, one launch (start us, length us, event | category | flops | bytes accessed | tf_op | source)
XLA Modules:
  0.0 55.7 jit_solution(17848790204235043251)
XLA Ops:
  0.0 52.5 %pair_block.1 = f32[32,128,128]{2,1,0:T(8,128)} custom-call(f32[32,128,128]{2,1,0:T(8,128)} %z_hbm.1, bf16[128,512]{1,0:T(8,128)(2,1)} %wqs.1, bf16[4,128]{1,0:T(4,128)(2,1)} %wbs.1, bf16[128,128]{1,0:T(8,128)(2,1)} %wos.1, bf16[128,512]{1,0:T(8,128)(2,1)} %wqe.1, bf16[4,128]{1,0:T(4,128)(2,1)} %wbe.1, bf16[128,128]{1,0:T(8,128)(2,1)} %woe.1, ...), custom_call_target="tpu_custom_call" | custom-call | tf_op jit(solution)/shard_map/pair_block/pallas_call | solution.py:268
  52.5 3.1 %copy.11 = f32[32,128,128]{2,1,0:T(8,128)} copy(f32[32,128,128]{2,1,0:T(8,128)} %pair_block.1) | data formatting | bytes 4194304
